TPU v7x, 32 devices: a whole 2x2x4 slice. The times are simulated.
32 devices in a mesh: dp: 16 (over z, x, core), mp: 2 (over y).
Axes of the slice: x: 2, y: 2, z: 4, core: 2. Of those that a mesh axis runs over, the one named last changes fastest.
Arguments:
- node_feats: bfloat16 [256, 32768], P('mp', 'dp'), may hold values from -6 to 6
- proj_weight: bfloat16 [256, 256], P('mp'), may hold values from -0.375 to 0.375
- att_src: float32 [256], P('mp'), may hold values from -32 to 32
- att_dst: float32 [256], P('mp'), may hold values from -32 to 32
- out_bias: float32 [256], P('mp'), may hold values from -3 to 3
- tile_rows: int32 [512], P('dp'), may hold values from 0 to 255, as said below
- tile_cols: int32 [512], P('dp'), may hold values from 0 to 255, as said below
- tile_masks: int32 [512, 4, 128], P('dp'), may hold values from -2147483648 to 2147483646
Outputs:
- node_out: bfloat16 [256, 32768], P('mp', 'dp')
Inputs may be any that keep to these rules, and one draw needn't show every extreme that they name: `tile_rows`: block b holds nodes 128 b to 128 b + 127 and belongs to index b // 16 of dp. Among the 32 tiles of one index of dp, no owner's blocks are named more than 4 times; on every index one owner's blocks are named exactly 4 times. `tile_cols`: the same bound holds for source blocks: among the 32 tiles of one index of dp, no owner's blocks are named more than 4 times, and one owner's exactly 4 times on every index.
All inputs are finite; a program needn't handle non-finite values.
Results may differ from a plain program's by a relative error of at most 0.0034.
Values may be sent and summed in bfloat16 or wider, within the bound.
No kernel may reach another device: no remote copies, remote signals or barrier semaphores. Data moves between devices by JAX's collectives and lax.ppermute only.
A program may use at most 64 MiB of HBM per device.

v0:
```python
import math
import jax
import jax.numpy as jnp
from jax import lax
from jax.sharding import PartitionSpec as P

HD = 32
far_below = -1e30


def leaky_relu(scores):
    return jnp.where(scores > 0, scores, 0.2 * scores)


def unpack_bits(packed):
    offsets = jnp.arange(32, dtype=jnp.int32)
    spread = jnp.bitwise_and(jnp.right_shift(packed[..., :, None, :], offsets[:, None]), 1)
    return spread.reshape(packed.shape[:-2] + (packed.shape[-2] * 32, packed.shape[-1]))


def edge_scores(edge_mask, source, target):
    raw_scores = leaky_relu(target[:, :, None, :] + source[:, :, :, None])
    return jnp.where(edge_mask[:, None] == 1, raw_scores, far_below)


def tile_group(inputs):
    packed, feats_here, source_here, target_here = inputs
    edge_mask = unpack_bits(packed)
    scores = edge_scores(edge_mask, source_here, target_here)
    tile_peaks = jnp.max(scores, axis=2)
    weights = jnp.where(edge_mask[:, None] == 1, jnp.exp(scores - tile_peaks[:, :, None, :]), 0.0)
    masses = jnp.sum(weights, axis=2)
    values = jnp.einsum(
        "ghdc,ghcr->ghdr",
        feats_here,
        weights.astype(jnp.bfloat16),
        preferred_element_type=jnp.float32,
    )
    return (tile_peaks, masses, values)


def local(node_feats, proj_weight, att_src, att_dst, out_bias, tile_rows, tile_cols, tile_masks):
    local_rows = node_feats.shape[1]
    head_dims = proj_weight.shape[0]
    local_heads = head_dims // HD
    tile_size = tile_masks.shape[2]
    local_blocks = local_rows // tile_size
    tile_count = tile_rows.shape[0]
    devices_dp = lax.axis_size("dp")
    capacity = max(2, 2 * tile_count // devices_dp)
    slot_count = devices_dp * capacity
    projected = jnp.dot(
        proj_weight,
        lax.all_gather(node_feats, "mp", axis=0, tiled=True),
        preferred_element_type=jnp.float32,
    )
    features = projected.astype(jnp.bfloat16)
    by_head = projected.reshape(local_heads, HD, local_rows)
    source = jnp.einsum(
        "hd,hdn->hn", att_src.reshape(local_heads, HD), by_head, precision=lax.Precision.HIGHEST
    )
    target = jnp.einsum(
        "hd,hdn->hn", att_dst.reshape(local_heads, HD), by_head, precision=lax.Precision.HIGHEST
    )
    source_blocks = source.reshape(local_heads, local_blocks, tile_size).transpose(1, 0, 2)
    target_blocks = target.reshape(local_heads, local_blocks, tile_size).transpose(1, 0, 2)
    feat_blocks = features.reshape(local_heads, HD, local_blocks, tile_size).transpose(2, 0, 1, 3)

    def slots_of(block_ids):
        owners = block_ids // local_blocks
        position = jnp.arange(tile_count, dtype=jnp.int32)
        earlier = (owners[:, None] == owners[None, :]) & (position[None, :] < position[:, None])
        return (owners * capacity + jnp.sum(earlier, axis=1), block_ids % local_blocks)

    def to_slots(slot_ids, entries):
        slot_hits = slot_ids[:, None] == jnp.arange(slot_count, dtype=jnp.int32)[None, :]
        return jnp.sum(jnp.where(slot_hits, entries[:, None], 0), axis=0).reshape(
            devices_dp, capacity
        )

    col_slot, col_local = slots_of(tile_cols)
    row_slot, row_local = slots_of(tile_rows)
    col_wanted = to_slots(col_slot, col_local)
    wanted, wanted_rows = (
        lax.all_to_all(col_wanted, "dp", split_axis=0, concat_axis=0, tiled=True),
        lax.all_to_all(
            to_slots(row_slot, row_local), "dp", split_axis=0, concat_axis=0, tiled=True
        ),
    )
    send_source = jnp.take(source_blocks, wanted.reshape(-1), axis=0).reshape(
        devices_dp, capacity, local_heads, tile_size
    )
    send_target = jnp.take(target_blocks, wanted_rows.reshape(-1), axis=0).reshape(
        devices_dp, capacity, local_heads, tile_size
    )
    got_source, got_target = (
        lax.all_to_all(send_source, "dp", split_axis=0, concat_axis=0, tiled=True),
        lax.all_to_all(send_target, "dp", split_axis=0, concat_axis=0, tiled=True),
    )
    tile_source = jnp.take(got_source.reshape(slot_count, local_heads, tile_size), col_slot, axis=0)
    tile_target = jnp.take(got_target.reshape(slot_count, local_heads, tile_size), row_slot, axis=0)
    send_feats = jnp.take(feat_blocks, wanted.reshape(-1), axis=0).reshape(
        devices_dp, capacity, local_heads, HD, tile_size
    )
    got_feats = lax.all_to_all(send_feats, "dp", split_axis=0, concat_axis=0, tiled=True)
    tile_feats = jnp.take(
        got_feats.reshape(slot_count, local_heads, HD, tile_size), col_slot, axis=0
    )
    group_size = math.gcd(tile_count, 8)

    def grouped(stacked):
        return stacked.reshape((tile_count // group_size, group_size) + stacked.shape[1:])

    tile_peaks, masses, values = lax.map(
        tile_group,
        (grouped(tile_masks), grouped(tile_feats), grouped(tile_source), grouped(tile_target)),
    )
    tile_peaks = tile_peaks.reshape(tile_count, local_heads, tile_size)
    masses = masses.reshape(tile_count, local_heads, tile_size)
    values = values.reshape(tile_count, local_heads, HD, tile_size)
    slot_hits = row_slot[:, None] == jnp.arange(slot_count, dtype=jnp.int32)[None, :]
    filled = jnp.any(slot_hits, axis=0)
    source_tile = jnp.sum(
        jnp.where(slot_hits, jnp.arange(tile_count, dtype=jnp.int32)[:, None], 0), axis=0
    )
    send_values = jnp.where(
        filled[:, None, None, None], jnp.take(values, source_tile, axis=0), 0.0
    ).reshape(devices_dp, capacity, local_heads, HD, tile_size)
    send_peaks = jnp.where(
        filled[:, None, None], jnp.take(tile_peaks, source_tile, axis=0), far_below
    ).reshape(devices_dp, capacity, local_heads, tile_size)
    send_masses = jnp.where(
        filled[:, None, None], jnp.take(masses, source_tile, axis=0), 0.0
    ).reshape(devices_dp, capacity, local_heads, tile_size)
    send_codes = (
        jnp.where(filled, jnp.take(row_local, source_tile), 0)
        .astype(jnp.float32)
        .reshape(devices_dp, capacity)
    )
    got_values, got_peaks, got_masses, got_codes = (
        lax.all_to_all(send_values, "dp", split_axis=0, concat_axis=0, tiled=True),
        lax.all_to_all(send_peaks, "dp", split_axis=0, concat_axis=0, tiled=True),
        lax.all_to_all(send_masses, "dp", split_axis=0, concat_axis=0, tiled=True),
        lax.all_to_all(send_codes, "dp", split_axis=0, concat_axis=0, tiled=True),
    )
    got_values = got_values.reshape(slot_count, local_heads, HD, tile_size)
    got_peaks = got_peaks.reshape(slot_count, local_heads, tile_size)
    got_masses = got_masses.reshape(slot_count, local_heads, tile_size)
    row_codes = got_codes.reshape(slot_count).astype(jnp.int32)
    self_scores = leaky_relu(source_blocks + target_blocks)
    row_peak = self_scores.at[row_codes].max(got_peaks)
    rescale = jnp.exp(got_peaks - row_peak[row_codes])
    self_weight = jnp.exp(self_scores - row_peak)
    denominator = self_weight.at[row_codes].add(rescale * got_masses)
    summed = (
        (self_weight[:, :, None, :] * feat_blocks.astype(jnp.float32))
        .at[row_codes]
        .add(rescale[:, :, None, :] * got_values)
    )
    gathered = summed / denominator[:, :, None, :]
    flat_out = gathered.transpose(1, 2, 0, 3).reshape(head_dims, local_rows)
    return jax.nn.elu(flat_out + node_feats.astype(jnp.float32) + out_bias[:, None]).astype(
        jnp.bfloat16
    )


def solution(mesh):
    return jax.shard_map(
        local,
        mesh=mesh,
        in_specs=(
            P("mp", "dp"),
            P("mp", None),
            P("mp"),
            P("mp"),
            P("mp"),
            P("dp"),
            P("dp"),
            P("dp", None, None),
        ),
        out_specs=P("mp", "dp"),
        check_vma=False,
    )
```

profile of v0, /device:TPU:11, one launch (start us, length us, event | category | flops | bytes accessed | tf_op | source)
XLA Modules:
  0.0 289.5 jit_solution(12951224629687775602)
XLA Ops:
  6.5 0.7 all-gather.2.cloned.1.call-update
  7.3 0.7 and_select_fusion.2
  8.8 0.7 all_to_all.35
  9.4 6.5 %all-to-all-start.1 = ((s32[16,1,4]{2,1,0:T(1,128)}), s32[16,1,4]{2,1,0:T(1,128)S(1)}, u32[]{:S(2)}, u32[]{:S(2)}) async-start(s32[16,1,4]{2,1,0:T(1,128)} %bitcast.21), calls=%async_computation.1 | async-start | bytes 16384 | tf_op jit(solution)/shard_map/all_to_all | solution.py:86
  16.0 0.7 and_select_fusion.1
  17.4 0.7 reshape.465
  18.2 0.7 reshape.467
  18.9 0.7 all_to_all.38
  19.8 6.0 %all-to-all-start.3 = ((s32[16,1,4]{2,1,0:T(1,128)}), s32[16,1,4]{2,1,0:T(1,128)S(1)}, u32[]{:S(2)}, u32[]{:S(2)}) async-start(s32[16,1,4]{2,1,0:T(1,128)} %bitcast.27), calls=%async_computation.3 | async-start | bytes 16384 | tf_op jit(solution)/shard_map/all_to_all | solution.py:85
  26.3 0.7 reduce.12
  27.0 2.7 all-to-all-done.3
  29.8 0.7 reduce.13
  31.4 1.5 fusion.30
  33.1 0.7 fusion.32
  33.8 0.7 gather_fusion.5
  34.4 0.8 broadcast_select_fusion.3
  35.2 6.2 %all-to-all-start.2 = ((f32[16,4,4,128]{3,2,1,0:T(4,128)}), f32[16,4,4,128]{3,2,1,0:T(4,128)S(1)}, u32[]{:S(2)}, u32[]{:S(2)}) async-start(f32[16,4,4,128]{3,2,1,0:T(4,128)} %bitcast.24), calls=%async_computation.2 | async-start | bytes 262144 | tf_op jit(solution)/shard_map/all_to_all | solution.py:98
  41.5 0.7 fusion.31
  42.4 0.7 gather_fusion.7
  43.1 1.0 gather_fusion.1
  44.0 1.4 broadcast_select_fusion.2
  45.5 1.1 all-to-all-done.2
  46.6 6.2 %all-to-all-start.4 = ((f32[16,4,4,128]{3,2,1,0:T(4,128)}), f32[16,4,4,128]{3,2,1,0:T(4,128)S(1)}, u32[]{:S(2)}, u32[]{:S(2)}) async-start(f32[16,4,4,128]{3,2,1,0:T(4,128)} %bitcast.30), calls=%async_computation.4 | async-start | bytes 262144 | tf_op jit(solution)/shard_map/all_to_all | solution.py:97
  52.8 1.5 broadcast_select_fusion
  54.4 3.6 %all-to-all-done.4 = f32[16,4,4,128]{3,2,1,0:T(4,128)S(1)} async-done(((f32[16,4,4,128]{3,2,1,0:T(4,128)}), f32[16,4,4,128]{3,2,1,0:T(4,128)S(1)}, u32[]{:S(2)}, u32[]{:S(2)}) %all-to-all-start.4) | async-done | bytes 131104 | tf_op jit(solution)/shard_map/all_to_all | solution.py:97
  58.0 7.0 %all-to-all-start.5 = ((bf16[16,4,4,32,128]{4,3,2,1,0:T(8,128)(2,1)}), bf16[16,4,4,32,128]{4,3,2,1,0:T(8,128)(2,1)}, u32[]{:S(2)}, u32[]{:S(2)}) async-start(bf16[16,4,4,32,128]{4,3,2,1,0:T(8,128)(2,1)} %broadcast_select_fusion), calls=%async_computation.5 | async-start | bytes 4194304 | tf_op jit(solution)/shard_map/all_to_all | solution.py:105
  65.6 0.8 gather_fusion
  66.6 0.7 copy.61
  68.8 43.8 %all-to-all-done.5 = bf16[16,4,4,32,128]{4,3,2,1,0:T(8,128)(2,1)} async-done(((bf16[16,4,4,32,128]{4,3,2,1,0:T(8,128)(2,1)}), bf16[16,4,4,32,128]{4,3,2,1,0:T(8,128)(2,1)}, u32[]{:S(2)}, u32[]{:S(2)}) %all-to-all-start.5) | async-done | bytes 2097184 | tf_op jit(solution)/shard_map/all_to_all | solution.py:105
  112.6 4.8 %all-to-all-start = ((f32[16,1,4]{2,1,0:T(1,128)}), f32[16,1,4]{2,1,0:T(1,128)S(1)}, u32[]{:S(2)}, u32[]{:S(2)}) async-start(f32[16,1,4]{2,1,0:T(1,128)} %copy.61), calls=%async_computation | async-start | bytes 16384 | tf_op jit(solution)/shard_map/all_to_all | solution.py:144
  117.3 3.3 %gather_fusion.2 = bf16[32,4,32,128]{3,2,1,0:T(8,128)(2,1)} fusion(bf16[64,4,32,128]{3,2,1,0:T(8,128)(2,1)} %bitcast.37, s32[1024]{0:T(1024)S(1)} %pad_clamp_fusion.3), kind=kCustom, calls=%fused_computation.8 | custom fusion | bytes 2097280 | tf_op jit(solution)/shard_map/jit(_take)/gather | solution.py:106
  120.6 2.4 broadcast_select_fusion.1
  123.0 18.8 %while.14 = (s32[]{:T(128)}, f32[4,8,4,128]{3,2,1,0:T(4,128)S(1)}, f32[4,8,4,128]{3,2,1,0:T(4,128)S(1)}, f32[4,8,4,32,128]{4,3,2,1,0:T(8,128)S(1)}, s32[4,8,4,12...) while((s32[]{:T(128)}, f32[4,8,4,128]{3,2,1,0:T(4,128)S(1)}, ...), condition=%wide.region_9.12_spmd, body=%wide.region_6.11_spmd.sunk | while | flops 45473792 | bytes 1657973 | solution.py:114
  123.1 0.7 dynamic-slice_bitcast_fusion.8
  124.0 0.7 fusion.48
  124.7 1.0 fusion.49
  125.7 1.9 fusion.50
  127.8 0.7 dynamic-slice_bitcast_fusion.8
  128.7 0.7 fusion.48
  129.4 1.0 fusion.49
  130.4 1.9 fusion.50
  132.5 0.7 dynamic-slice_bitcast_fusion.8
  133.4 0.7 fusion.48
  134.1 1.0 fusion.49
  135.1 1.9 fusion.50
  137.2 0.7 dynamic-slice_bitcast_fusion.8
  138.1 0.7 fusion.48
  138.8 1.0 fusion.49
  139.8 1.9 fusion.50
  141.8 0.7 gather_fusion.9
  142.5 0.7 gather_fusion.10
  143.1 0.9 select_select_fusion.1
  144.0 6.0 %all-to-all-start.6 = ((f32[16,4,4,128]{3,2,1,0:T(4,128)}), f32[16,4,4,128]{3,2,1,0:T(4,128)S(1)}, u32[]{:S(2)}, u32[]{:S(2)}) async-start(f32[16,4,4,128]{3,2,1,0:T(4,128)} %bitcast.40), calls=%async_computation.6 | async-start | bytes 262144 | tf_op jit(solution)/shard_map/all_to_all | solution.py:142
  150.4 2.8 gather_fusion.4
  153.2 2.0 all-to-all-done.6
  155.2 6.2 %all-to-all-start.8 = ((f32[16,4,4,128]{3,2,1,0:T(4,128)}), f32[16,4,4,128]{3,2,1,0:T(4,128)S(1)}, u32[]{:S(2)}, u32[]{:S(2)}) async-start(f32[16,4,4,128]{3,2,1,0:T(4,128)} %bitcast.46), calls=%async_computation.8 | async-start | bytes 262144 | tf_op jit(solution)/shard_map/all_to_all | solution.py:143
  161.4 4.7 %select_select_fusion = f32[16,4,4,32,128]{4,3,2,1,0:T(8,128)} fusion(f32[16,4,4,32,128]{4,3,2,1,0:T(8,128)} %bitcast.127, pred[16,4]{1,0:T(8,128)(4,1)S(1)} %copy.70, pred[16,4]{1,0:T(8,128)(4,1)S(1)} %broadcast_in_dim.205), kind=kLoop, calls=%fused_computation.44 | loop fusion | flops 2097152 | bytes 8388736 | tf_op jit(solution)/shard_map/jit(_where)/select_n | solution.py:126
  166.6 7.1 %all-to-all-start.7 = ((f32[16,4,4,32,128]{4,3,2,1,0:T(8,128)}), f32[16,4,4,32,128]{4,3,2,1,0:T(8,128)}, u32[]{:S(2)}, u32[]{:S(2)}) async-start(f32[16,4,4,32,128]{4,3,2,1,0:T(8,128)} %select_select_fusion), calls=%async_computation.7 | async-start | bytes 8388608 | tf_op jit(solution)/shard_map/all_to_all | solution.py:141
  173.9 2.8 scatter_fusion
  177.7 2.8 scatter_fusion.2
  180.5 85.7 %all-to-all-done.7 = f32[16,4,4,32,128]{4,3,2,1,0:T(8,128)} async-done(((f32[16,4,4,32,128]{4,3,2,1,0:T(8,128)}), f32[16,4,4,32,128]{4,3,2,1,0:T(8,128)}, u32[]{:S(2)}, u32[]{:S(2)}) %all-to-all-start.7) | async-done | bytes 4194336 | tf_op jit(solution)/shard_map/all_to_all | solution.py:141
  266.2 5.1 %bitcast_multiply_fusion = f32[64,4,32,128]{3,2,1,0:T(8,128)} fusion(f32[16,4,4,32,128]{4,3,2,1,0:T(8,128)} %all-to-all-done.7, f32[64,4,128]{2,1,0:T(4,128)S(1)} %get-tuple-element.74), kind=kLoop, calls=%fused_computation.43 | loop fusion | flops 1048576 | bytes 8519680 | tf_op jit(solution)/shard_map/mul | solution.py:158
  271.3 8.8 %scatter_fusion.1 = f32[16,4,32,128]{3,2,1,0:T(8,128)S(1)} fusion(f32[16,4,32,128]{3,2,1,0:T(8,128)S(1)} %convert_multiply_fusion, s32[64]{0:T(128)S(1)} %fusion.28, f32[64,4,32,128]{3,2,1,0:T(8,128)} %bitcast_multiply_fusion), kind=kCustom, calls=%fused_computation.12 | custom fusion | flops 1048576 | bytes 12583168 | tf_op jit(solution)/shard_map/scatter-add | solution.py:158
  281.2 1.4 fusion.22
  (114 shorter events, 10.1 us)
Async XLA Ops:
  6.5 24.9 %copy-start = (bf16[128,256]{1,0:T(8,128)(2,1)S(1)}, bf16[128,256]{1,0:T(8,128)(2,1)}, u32[]{:S(2)}) copy-start(bf16[128,256]{1,0:T(8,128)(2,1)} %param.17) | copy-start | bytes 196612
  6.5 24.9 %all-gather.2.cloned.1.call-start = ((), (), s32[]{:S(2)}) async-start(), calls=%async_computation.9 | async-start | bytes 1572864 | tf_op jit(solution)/shard_map/all_gather | solution.py:54
  8.7 11.1 %copy-start.4 = (s32[32]{0:T(128)}, s32[32]{0:T(128)S(1)}, u32[]{:S(2)}) copy-start(s32[32]{0:T(128)S(1)} %get-tuple-element.78) | copy-start | bytes 388
  9.4 10.3 %all-to-all-start.1 = ((s32[16,1,4]{2,1,0:T(1,128)}), s32[16,1,4]{2,1,0:T(1,128)S(1)}, u32[]{:S(2)}, u32[]{:S(2)}) async-start(s32[16,1,4]{2,1,0:T(1,128)} %bitcast.21), calls=%async_computation.1 | async-start | bytes 16384 | tf_op jit(solution)/shard_map/all_to_all | solution.py:86
  17.3 8.4 %copy-start.7 = (s32[32]{0:T(128)}, s32[32]{0:T(128)S(1)}, u32[]{:S(2)}) copy-start(s32[32]{0:T(128)S(1)} %get-tuple-element.76) | copy-start | bytes 388
  19.8 9.9 %all-to-all-start.3 = ((s32[16,1,4]{2,1,0:T(1,128)}), s32[16,1,4]{2,1,0:T(1,128)S(1)}, u32[]{:S(2)}, u32[]{:S(2)}) async-start(s32[16,1,4]{2,1,0:T(1,128)} %bitcast.27), calls=%async_computation.3 | async-start | bytes 16384 | tf_op jit(solution)/shard_map/all_to_all | solution.py:85
  35.2 11.4 %all-to-all-start.2 = ((f32[16,4,4,128]{3,2,1,0:T(4,128)}), f32[16,4,4,128]{3,2,1,0:T(4,128)S(1)}, u32[]{:S(2)}, u32[]{:S(2)}) async-start(f32[16,4,4,128]{3,2,1,0:T(4,128)} %bitcast.24), calls=%async_computation.2 | async-start | bytes 262144 | tf_op jit(solution)/shard_map/all_to_all | solution.py:98
  46.6 11.4 %all-to-all-start.4 = ((f32[16,4,4,128]{3,2,1,0:T(4,128)}), f32[16,4,4,128]{3,2,1,0:T(4,128)S(1)}, u32[]{:S(2)}, u32[]{:S(2)}) async-start(f32[16,4,4,128]{3,2,1,0:T(4,128)} %bitcast.30), calls=%async_computation.4 | async-start | bytes 262144 | tf_op jit(solution)/shard_map/all_to_all | solution.py:97
  54.3 10.7 %copy-start.3 = (pred[32]{0:T(512)(128)(4,1)S(1)}, pred[32]{0:T(512)(128)(4,1)}, u32[]{:S(2)}) copy-start(pred[32]{0:T(512)(128)(4,1)} %get-tuple-element.75) | copy-start | bytes 100
  54.3 10.8 %copy-start.5 = (s32[32]{0:T(128)S(1)}, s32[32]{0:T(128)}, u32[]{:S(2)}) copy-start(s32[32]{0:T(128)} %copy-done.4) | copy-start | bytes 388
  54.3 12.9 %copy-start.8 = (s32[32]{0:T(128)S(1)}, s32[32]{0:T(128)}, u32[]{:S(2)}) copy-start(s32[32]{0:T(128)} %copy-done.7) | copy-start | bytes 388
  54.4 14.3 %copy-start.2 = (pred[32]{0:T(512)(128)(4,1)S(1)}, pred[32]{0:T(512)(128)(4,1)}, u32[]{:S(2)}) copy-start(pred[32]{0:T(512)(128)(4,1)} %get-tuple-element.77) | copy-start | bytes 100
  58.0 54.6 %all-to-all-start.5 = ((bf16[16,4,4,32,128]{4,3,2,1,0:T(8,128)(2,1)}), bf16[16,4,4,32,128]{4,3,2,1,0:T(8,128)(2,1)}, u32[]{:S(2)}, u32[]{:S(2)}) async-start(bf16[16,4,4,32,128]{4,3,2,1,0:T(8,128)(2,1)} %broadcast_select_fusion), calls=%async_computation.5 | async-start | bytes 4194304 | tf_op jit(solution)/shard_map/all_to_all | solution.py:105
  112.6 31.4 %all-to-all-start = ((f32[16,1,4]{2,1,0:T(1,128)}), f32[16,1,4]{2,1,0:T(1,128)S(1)}, u32[]{:S(2)}, u32[]{:S(2)}) async-start(f32[16,1,4]{2,1,0:T(1,128)} %copy.61), calls=%async_computation | async-start | bytes 16384 | tf_op jit(solution)/shard_map/all_to_all | solution.py:144
  144.0 11.2 %all-to-all-start.6 = ((f32[16,4,4,128]{3,2,1,0:T(4,128)}), f32[16,4,4,128]{3,2,1,0:T(4,128)S(1)}, u32[]{:S(2)}, u32[]{:S(2)}) async-start(f32[16,4,4,128]{3,2,1,0:T(4,128)} %bitcast.40), calls=%async_computation.6 | async-start | bytes 262144 | tf_op jit(solution)/shard_map/all_to_all | solution.py:142
  155.2 11.4 %all-to-all-start.8 = ((f32[16,4,4,128]{3,2,1,0:T(4,128)}), f32[16,4,4,128]{3,2,1,0:T(4,128)S(1)}, u32[]{:S(2)}, u32[]{:S(2)}) async-start(f32[16,4,4,128]{3,2,1,0:T(4,128)} %bitcast.46), calls=%async_computation.8 | async-start | bytes 262144 | tf_op jit(solution)/shard_map/all_to_all | solution.py:143
  166.6 99.6 %all-to-all-start.7 = ((f32[16,4,4,32,128]{4,3,2,1,0:T(8,128)}), f32[16,4,4,32,128]{4,3,2,1,0:T(8,128)}, u32[]{:S(2)}, u32[]{:S(2)}) async-start(f32[16,4,4,32,128]{4,3,2,1,0:T(8,128)} %select_select_fusion), calls=%async_computation.7 | async-start | bytes 8388608 | tf_op jit(solution)/shard_map/all_to_all | solution.py:141
  280.1 1.0 copy-start.1
  280.1 1.0 copy-start.6
Sparse Core Ops, SparseCore 0:
  8.9 22.2 all-gather.1
where the time goes:
time: 291 us; the launch traced here: 289 us
  waiting for transfers between devices  140 us (48%)
  starting transfers between devices  56.1 us (19%)
  other arithmetic  46.2 us (16%)
  local copies, waits for them, and re-layouts  22.2 us (8%)
  between operations  13.8 us (5%)
  matrix products  10.6 us (4%)
    all_to_all x1, waiting for transfers between devices, local(): lax.all_to_all(send_values, 'dp', split_axis=0, concat_axis=0, tiled=True)  85.7 us
    all_to_all x1, waiting for transfers between devices, local(): lax.all_to_all(send_feats, 'dp', split_axis=0, concat_axis=0, tiled=True)  43.8 us
    scatter-add x1, other arithmetic, local(): summed = (self_weight[:, :, None, :] * feat_blocks.astype(jnp.float32)).a...  8.79 us
    dot_general x4, matrix products, tile_group(): jnp.einsum('ghdc,ghcr->ghdr', feats_here, weights.astype(jnp.bfloat16), p...  7.77 us
    all_to_all x1, starting transfers between devices, local(): lax.all_to_all(send_values, 'dp', split_axis=0, concat_axis=0, tiled=True)  7.15 us
    all_to_all x1, starting transfers between devices, local(): lax.all_to_all(send_feats, 'dp', split_axis=0, concat_axis=0, tiled=True)  7.04 us
    all_to_all x1, starting transfers between devices, local(): lax.all_to_all(to_slots(row_slot, row_local), 'dp', split_axis=0, concat_...  6.52 us
    all_to_all x1, starting transfers between devices, local(): lax.all_to_all(send_target, 'dp', split_axis=0, concat_axis=0, tiled=True)  6.25 us
  transfers between devices with their start and end apart: 10, of which 8 were waited for; matrix products, arithmetic and copies ran while one was open for 20% of the time, Pallas kernels for 0%

commit v1 on v0

--- a/solution.py
+++ b/solution.py
@@ -6,6 +6,22 @@
 
 HD = 32
 far_below = -1e30
+
+
+def exchange_in_pairs(x, axis, split, join):
+    ways, here = (lax.axis_size(axis), lax.axis_index(axis))
+    width = x.shape[split] // ways
+    lengths = list(x.shape)
+    lengths[split] = width
+    height = lengths[join]
+    lengths[join] = height * ways
+    full = jnp.zeros(lengths, x.dtype)
+    for mask in range(ways):
+        part = lax.dynamic_slice_in_dim(x, (here ^ mask) * width, width, axis=split)
+        if mask:
+            part = lax.ppermute(part, axis, [(d, d ^ mask) for d in range(ways)])
+        full = lax.dynamic_update_slice_in_dim(full, part, (here ^ mask) * height, axis=join)
+    return full
 
 
 def leaky_relu(scores):
@@ -102,7 +118,7 @@
     send_feats = jnp.take(feat_blocks, wanted.reshape(-1), axis=0).reshape(
         devices_dp, capacity, local_heads, HD, tile_size
     )
-    got_feats = lax.all_to_all(send_feats, "dp", split_axis=0, concat_axis=0, tiled=True)
+    got_feats = exchange_in_pairs(send_feats, "dp", 0, 0)
     tile_feats = jnp.take(
         got_feats.reshape(slot_count, local_heads, HD, tile_size), col_slot, axis=0
     )

time: 291 us -> 305 us (1.048)
  waiting for transfers between devices: 140 us -> 110 us
  starting transfers between devices: 56.1 us -> 82.6 us
  local copies, waits for them, and re-layouts: 22.2 us -> 41.7 us
    all_to_all x1 -> x0, waiting for transfers between devices: 43.8 us -> none  [local(): lax.all_to_all(send_feats, 'dp', split_axis=0, concat_axis=0, tiled=True)]
    ppermute x0 -> x15, starting transfers between devices: none -> 30.1 us  [exchange_in_pairs(): part = lax.ppermute(part, axis, [(d, d ^ mask) for d in range(ways)])]
    ppermute x0 -> x15, waiting for transfers between devices: none -> 14.9 us  [exchange_in_pairs(): part = lax.ppermute(part, axis, [(d, d ^ mask) for d in range(ways)])]
    dynamic_update_slice x0 -> x15, local copies, waits for them, and re-layouts: none -> 14.4 us  [exchange_in_pairs(): lax.dynamic_update_slice_in_dim(full, part, (here ^ mask) * height, axis=...]
    all_to_all x1 -> x0, starting transfers between devices: 7.04 us -> none  [local(): lax.all_to_all(send_feats, 'dp', split_axis=0, concat_axis=0, tiled=True)]
    all_to_all x1, waiting for transfers between devices: 3.65 us -> 0.01 us  [local(): lax.all_to_all(send_source, 'dp', split_axis=0, concat_axis=0, tiled=True)]
    all_to_all x1, waiting for transfers between devices: 0.16 us -> 3.77 us  [local(): lax.all_to_all(to_slots(row_slot, row_local), 'dp', split_axis=0, concat_...]
  transfers between devices with their start and end apart: 10 -> 24, of which waited for: 8 -> 13; matrix products, arithmetic and copies ran while one was open for 20% -> 24% of each run, Pallas kernels for 0% -> 0%
where the time goes in v1:
time: 305 us; the launch traced here: 304 us
  waiting for transfers between devices  110 us (36%)
  starting transfers between devices  82.6 us (27%)
  other arithmetic  44.6 us (15%)
  local copies, waits for them, and re-layouts  41.7 us (14%)
  between operations  13.8 us (5%)
  matrix products  10.6 us (3%)
    all_to_all x1, waiting for transfers between devices, local(): lax.all_to_all(send_values, 'dp', split_axis=0, concat_axis=0, tiled=True)  85.7 us
    ppermute x15, starting transfers between devices, exchange_in_pairs(): part = lax.ppermute(part, axis, [(d, d ^ mask) for d in range(ways)])  30.1 us
    ppermute x15, waiting for transfers between devices, exchange_in_pairs(): part = lax.ppermute(part, axis, [(d, d ^ mask) for d in range(ways)])  14.9 us
    dynamic_update_slice x15, local copies, waits for them, and re-layouts, exchange_in_pairs(): lax.dynamic_update_slice_in_dim(full, part, (here ^ mask) * height, axis=...  14.4 us
    scatter-add x1, other arithmetic, local(): summed = (self_weight[:, :, None, :] * feat_blocks.astype(jnp.float32)).a...  8.79 us
    all_to_all x1, starting transfers between devices, local(): lax.all_to_all(send_target, 'dp', split_axis=0, concat_axis=0, tiled=True)  8.43 us
    dot_general x4, matrix products, tile_group(): jnp.einsum('ghdc,ghcr->ghdr', feats_here, weights.astype(jnp.bfloat16), p...  7.77 us
    all_to_all x1, starting transfers between devices, local(): lax.all_to_all(send_values, 'dp', split_axis=0, concat_axis=0, tiled=True)  7.15 us
  transfers between devices with their start and end apart: 24, of which 13 were waited for; matrix products, arithmetic and copies ran while one was open for 24% of the time, Pallas kernels for 0%

profile of v1, /device:TPU:11, one launch (start us, length us, event | category | flops | bytes accessed | tf_op | source)
XLA Modules:
  0.0 303.6 jit_solution(13165555043327714131)
XLA Ops:
  8.9 6.5 %all-to-all-start.3 = ((s32[16,1,4]{2,1,0:T(1,128)}), s32[16,1,4]{2,1,0:T(1,128)S(1)}, u32[]{:S(2)}, u32[]{:S(2)}) async-start(s32[16,1,4]{2,1,0:T(1,128)} %bitcast.27), calls=%async_computation.3 | async-start | bytes 16384 | tf_op jit(solution)/shard_map/all_to_all | solution.py:101
  18.1 0.8 reshape.465
  19.6 0.8 gather_fusion
  22.1 6.0 %all-to-all-start.1 = ((s32[16,1,4]{2,1,0:T(1,128)}), s32[16,1,4]{2,1,0:T(1,128)S(1)}, u32[]{:S(2)}, u32[]{:S(2)}) async-start(s32[16,1,4]{2,1,0:T(1,128)} %bitcast.21), calls=%async_computation.1 | async-start | bytes 16384 | tf_op jit(solution)/shard_map/all_to_all | solution.py:102
  28.2 3.8 %all-to-all-done.1 = s32[16,1,4]{2,1,0:T(1,128)S(1)} async-done(((s32[16,1,4]{2,1,0:T(1,128)}), s32[16,1,4]{2,1,0:T(1,128)S(1)}, u32[]{:S(2)}, u32[]{:S(2)}) %all-to-all-start.1) | async-done | bytes 288 | tf_op jit(solution)/shard_map/all_to_all | solution.py:102
  34.3 1.5 fusion.30
  38.0 0.8 broadcast_select_fusion.2
  38.8 6.0 %all-to-all-start.4 = ((f32[16,4,4,128]{3,2,1,0:T(4,128)}), f32[16,4,4,128]{3,2,1,0:T(4,128)S(1)}, u32[]{:S(2)}, u32[]{:S(2)}) async-start(f32[16,4,4,128]{3,2,1,0:T(4,128)} %bitcast.30), calls=%async_computation.4 | async-start | bytes 262144 | tf_op jit(solution)/shard_map/all_to_all | solution.py:113
  45.1 2.1 gather_fusion.1
  47.2 1.8 broadcast_select_fusion
  49.6 1.4 constant_dynamic-slice_fusion
  51.0 1.3 copy-done.1
  52.4 1.5 collective-permute-start.14
  53.8 1.2 collective-permute-start.13
  55.0 1.5 collective-permute-start.12
  57.8 0.8 broadcast_select_fusion.3
  58.6 1.3 collective-permute-start.2
  59.9 1.6 constant_dynamic-update-slice_fusion.14
  61.9 5.0 %collective-permute-start.3 = (bf16[1,4,4,32,128]{4,3,2,1,0:T(8,128)(2,1)}, bf16[1,4,4,32,128]{4,3,2,1,0:T(8,128)(2,1)S(1)}, u32[]{:S(2)}, u32[]{:S(2)}) collective-permute-start(bf16[1,4,4,32,128]{4,3,2,1,0:T(8,128)(2,1)} %get-tuple-element.92), channel_id=1, source_target_pairs={{0,8},{2,10},{4,12},{6,14},{8,0},{10,2},{12,4},{14,6},{16,24},{18,... | collective-permute-start | bytes 393224 | tf_op jit(solution)/shard_map/ppermute | solution.py:22
  66.9 1.6 constant_dynamic-update-slice_fusion.13
  68.5 1.4 collective-permute-start.4
  70.6 2.2 collective-permute-start.5
  73.4 1.1 collective-permute-done.4
  74.5 2.2 collective-permute-start.6
  77.4 1.3 collective-permute-done.5
  79.7 2.0 collective-permute-done.6
  81.7 2.1 collective-permute-start.8
  84.8 8.2 %collective-permute-start.9 = (bf16[1,4,4,32,128]{4,3,2,1,0:T(8,128)(2,1)S(1)}, bf16[1,4,4,32,128]{4,3,2,1,0:T(8,128)(2,1)S(1)}, u32[]{:S(2)}, u32[]{:S(2)}) collective-permute-start(bf16[1,4,4,32,128]{4,3,2,1,0:T(8,128)(2,1)S(1)} %copy-done.6), channel_id=1, source_target_pairs={{0,20},{2,22},{4,16},{6,18},{8,28},{10,30},{12,24},{14,26},{16,4},... | collective-permute-start | bytes 393224 | tf_op jit(solution)/shard_map/ppermute | solution.py:22
  93.6 2.5 collective-permute-start.10
  96.8 1.0 collective-permute-done.9
  98.5 3.7 %collective-permute-done.10 = bf16[1,4,4,32,128]{4,3,2,1,0:T(8,128)(2,1)S(1)} collective-permute-done((bf16[1,4,4,32,128]{4,3,2,1,0:T(8,128)(2,1)S(1)}, bf16[1,4,4,32,128]{4,3,2,1,0:T(8,128)(2,1)S(1)}, u32[]{:S(2)}, u32[]{:S(2)}) %collective-permute-start.10) | collective-permute-done | bytes 131104 | tf_op jit(solution)/shard_map/ppermute | solution.py:22
  102.8 5.1 %collective-permute-done.11 = bf16[1,4,4,32,128]{4,3,2,1,0:T(8,128)(2,1)S(1)} collective-permute-done((bf16[1,4,4,32,128]{4,3,2,1,0:T(8,128)(2,1)S(1)}, bf16[1,4,4,32,128]{4,3,2,1,0:T(8,128)(2,1)S(1)}, u32[]{:S(2)}, u32[]{:S(2)}) %collective-permute-start.11) | collective-permute-done | bytes 131104 | tf_op jit(solution)/shard_map/ppermute | solution.py:22
  108.6 1.6 constant_dynamic-update-slice_fusion.2
  110.1 1.6 constant_dynamic-update-slice_fusion.1
  111.7 1.6 constant_dynamic-update-slice_fusion
  113.3 3.3 %gather_fusion.2 = bf16[32,4,32,128]{3,2,1,0:T(8,128)(2,1)} fusion(bf16[64,4,32,128]{3,2,1,0:T(8,128)(2,1)} %bitcast.131, s32[1024]{0:T(1024)S(1)} %pad_clamp_fusion.3), kind=kCustom, calls=%fused_computation.8 | custom fusion | bytes 2097280 | tf_op jit(solution)/shard_map/jit(_take)/gather | solution.py:122
  116.5 8.4 %all-to-all-start.2 = ((f32[16,4,4,128]{3,2,1,0:T(4,128)}), f32[16,4,4,128]{3,2,1,0:T(4,128)S(1)}, u32[]{:S(2)}, u32[]{:S(2)}) async-start(f32[16,4,4,128]{3,2,1,0:T(4,128)} %bitcast.24), calls=%async_computation.2 | async-start | bytes 262144 | tf_op jit(solution)/shard_map/all_to_all | solution.py:114
  125.0 2.4 broadcast_select_fusion.1
  128.0 2.1 all-to-all-done.2
  130.1 6.1 %all-to-all-start = ((f32[16,1,4]{2,1,0:T(1,128)}), f32[16,1,4]{2,1,0:T(1,128)S(1)}, u32[]{:S(2)}, u32[]{:S(2)}) async-start(f32[16,1,4]{2,1,0:T(1,128)} %copy.61), calls=%async_computation | async-start | bytes 16384 | tf_op jit(solution)/shard_map/all_to_all | solution.py:160
  137.0 18.8 %while.14 = (s32[]{:T(128)}, f32[4,8,4,128]{3,2,1,0:T(4,128)S(1)}, f32[4,8,4,128]{3,2,1,0:T(4,128)S(1)}, f32[4,8,4,32,128]{4,3,2,1,0:T(8,128)S(1)}, s32[4,8,4,12...) while((s32[]{:T(128)}, f32[4,8,4,128]{3,2,1,0:T(4,128)S(1)}, ...), condition=%wide.region_9.12_spmd, body=%wide.region_6.11_spmd.sunk | while | flops 45473792 | bytes 1657973 | solution.py:130
  138.0 0.7 fusion.48
  138.7 1.0 fusion.49
  139.8 1.9 fusion.50
  142.7 0.7 fusion.48
  143.5 1.0 fusion.49
  144.5 1.9 fusion.50
  148.2 1.0 fusion.49
  149.2 1.9 fusion.50
  152.9 1.0 fusion.49
  153.9 1.9 fusion.50
  157.2 0.9 select_select_fusion.1
  158.1 6.1 %all-to-all-start.5 = ((f32[16,4,4,128]{3,2,1,0:T(4,128)}), f32[16,4,4,128]{3,2,1,0:T(4,128)S(1)}, u32[]{:S(2)}, u32[]{:S(2)}) async-start(f32[16,4,4,128]{3,2,1,0:T(4,128)} %bitcast.40), calls=%async_computation.5 | async-start | bytes 262144 | tf_op jit(solution)/shard_map/all_to_all | solution.py:158
  164.3 2.8 gather_fusion.4
  167.1 2.2 all-to-all-done.5
  169.3 6.2 %all-to-all-start.7 = ((f32[16,4,4,128]{3,2,1,0:T(4,128)}), f32[16,4,4,128]{3,2,1,0:T(4,128)S(1)}, u32[]{:S(2)}, u32[]{:S(2)}) async-start(f32[16,4,4,128]{3,2,1,0:T(4,128)} %bitcast.46), calls=%async_computation.7 | async-start | bytes 262144 | tf_op jit(solution)/shard_map/all_to_all | solution.py:159
  175.5 4.6 %select_select_fusion = f32[16,4,4,32,128]{4,3,2,1,0:T(8,128)} fusion(f32[16,4,4,32,128]{4,3,2,1,0:T(8,128)} %bitcast.127, pred[16,4]{1,0:T(8,128)(4,1)S(1)} %copy.70, pred[16,4]{1,0:T(8,128)(4,1)S(1)} %broadcast_in_dim.209), kind=kLoop, calls=%fused_computation.44 | loop fusion | flops 2097152 | bytes 8388736 | tf_op jit(solution)/shard_map/jit(_where)/select_n | solution.py:142
  180.7 7.2 %all-to-all-start.6 = ((f32[16,4,4,32,128]{4,3,2,1,0:T(8,128)}), f32[16,4,4,32,128]{4,3,2,1,0:T(8,128)}, u32[]{:S(2)}, u32[]{:S(2)}) async-start(f32[16,4,4,32,128]{4,3,2,1,0:T(8,128)} %select_select_fusion), calls=%async_computation.6 | async-start | bytes 8388608 | tf_op jit(solution)/shard_map/all_to_all | solution.py:157
  188.0 2.8 scatter_fusion
  191.8 2.8 scatter_fusion.2
  194.6 85.7 %all-to-all-done.6 = f32[16,4,4,32,128]{4,3,2,1,0:T(8,128)} async-done(((f32[16,4,4,32,128]{4,3,2,1,0:T(8,128)}), f32[16,4,4,32,128]{4,3,2,1,0:T(8,128)}, u32[]{:S(2)}, u32[]{:S(2)}) %all-to-all-start.6) | async-done | bytes 4194336 | tf_op jit(solution)/shard_map/all_to_all | solution.py:157
  280.3 5.1 %bitcast_multiply_fusion = f32[64,4,32,128]{3,2,1,0:T(8,128)} fusion(f32[16,4,4,32,128]{4,3,2,1,0:T(8,128)} %all-to-all-done.6, f32[64,4,128]{2,1,0:T(4,128)S(1)} %get-tuple-element.74), kind=kLoop, calls=%fused_computation.43 | loop fusion | flops 1048576 | bytes 8519680 | tf_op jit(solution)/shard_map/mul | solution.py:174
  285.4 8.8 %scatter_fusion.1 = f32[16,4,32,128]{3,2,1,0:T(8,128)S(1)} fusion(f32[16,4,32,128]{3,2,1,0:T(8,128)S(1)} %convert_multiply_fusion, s32[64]{0:T(128)S(1)} %fusion.28, f32[64,4,32,128]{3,2,1,0:T(8,128)} %bitcast_multiply_fusion), kind=kCustom, calls=%fused_computation.12 | custom fusion | flops 1048576 | bytes 12583168 | tf_op jit(solution)/shard_map/scatter-add | solution.py:174
  295.3 1.4 fusion.22
  (158 shorter events, 32.7 us)
Async XLA Ops:
  6.5 27.8 %copy-start = (bf16[128,256]{1,0:T(8,128)(2,1)S(1)}, bf16[128,256]{1,0:T(8,128)(2,1)}, u32[]{:S(2)}) copy-start(bf16[128,256]{1,0:T(8,128)(2,1)} %param.17) | copy-start | bytes 196612
  6.5 27.8 %all-gather.2.cloned.1.call-start = ((), (), s32[]{:S(2)}) async-start(), calls=%async_computation.8 | async-start | bytes 1572864 | tf_op jit(solution)/shard_map/all_gather | solution.py:70
  8.9 13.2 %all-to-all-start.3 = ((s32[16,1,4]{2,1,0:T(1,128)}), s32[16,1,4]{2,1,0:T(1,128)S(1)}, u32[]{:S(2)}, u32[]{:S(2)}) async-start(s32[16,1,4]{2,1,0:T(1,128)} %bitcast.27), calls=%async_computation.3 | async-start | bytes 16384 | tf_op jit(solution)/shard_map/all_to_all | solution.py:101
  22.1 9.9 %all-to-all-start.1 = ((s32[16,1,4]{2,1,0:T(1,128)}), s32[16,1,4]{2,1,0:T(1,128)S(1)}, u32[]{:S(2)}, u32[]{:S(2)}) async-start(s32[16,1,4]{2,1,0:T(1,128)} %bitcast.21), calls=%async_computation.1 | async-start | bytes 16384 | tf_op jit(solution)/shard_map/all_to_all | solution.py:102
  38.8 77.7 %all-to-all-start.4 = ((f32[16,4,4,128]{3,2,1,0:T(4,128)}), f32[16,4,4,128]{3,2,1,0:T(4,128)S(1)}, u32[]{:S(2)}, u32[]{:S(2)}) async-start(f32[16,4,4,128]{3,2,1,0:T(4,128)} %bitcast.30), calls=%async_computation.4 | async-start | bytes 262144 | tf_op jit(solution)/shard_map/all_to_all | solution.py:113
  51.0 1.3 copy-start.1
  52.4 59.3 %collective-permute-start.14 = (bf16[1,4,4,32,128]{4,3,2,1,0:T(8,128)(2,1)S(1)}, bf16[1,4,4,32,128]{4,3,2,1,0:T(8,128)(2,1)}, u32[]{:S(2)}, u32[]{:S(2)}) collective-permute-start(bf16[1,4,4,32,128]{4,3,2,1,0:T(8,128)(2,1)S(1)} %get-tuple-element.81), channel_id=1, source_target_pairs={{0,30},{2,28},{4,26},{6,24},{8,22},{10,20},{12,18},{14,16},{16,14}... | collective-permute-start | bytes 393224 | tf_op jit(solution)/shard_map/ppermute | solution.py:22
  53.8 56.3 %collective-permute-start.13 = (bf16[1,4,4,32,128]{4,3,2,1,0:T(8,128)(2,1)S(1)}, bf16[1,4,4,32,128]{4,3,2,1,0:T(8,128)(2,1)}, u32[]{:S(2)}, u32[]{:S(2)}) collective-permute-start(bf16[1,4,4,32,128]{4,3,2,1,0:T(8,128)(2,1)S(1)} %get-tuple-element.82), channel_id=1, source_target_pairs={{0,28},{2,30},{4,24},{6,26},{8,20},{10,22},{12,16},{14,18},{16,12}... | collective-permute-start | bytes 393224 | tf_op jit(solution)/shard_map/ppermute | solution.py:22
  55.0 53.6 %collective-permute-start.12 = (bf16[1,4,4,32,128]{4,3,2,1,0:T(8,128)(2,1)S(1)}, bf16[1,4,4,32,128]{4,3,2,1,0:T(8,128)(2,1)}, u32[]{:S(2)}, u32[]{:S(2)}) collective-permute-start(bf16[1,4,4,32,128]{4,3,2,1,0:T(8,128)(2,1)S(1)} %get-tuple-element.83), channel_id=1, source_target_pairs={{0,26},{2,24},{4,30},{6,28},{8,18},{10,16},{12,22},{14,20},{16,10}... | collective-permute-start | bytes 393224 | tf_op jit(solution)/shard_map/ppermute | solution.py:22
  56.5 5.4 %collective-permute-start.1 = (bf16[1,4,4,32,128]{4,3,2,1,0:T(8,128)(2,1)}, bf16[1,4,4,32,128]{4,3,2,1,0:T(8,128)(2,1)}, u32[]{:S(2)}, u32[]{:S(2)}) collective-permute-start(bf16[1,4,4,32,128]{4,3,2,1,0:T(8,128)(2,1)} %get-tuple-element.94), channel_id=1, source_target_pairs={{0,4},{2,6},{4,0},{6,2},{8,12},{10,14},{12,8},{14,10},{16,20},{18,... | collective-permute-start | bytes 393224 | tf_op jit(solution)/shard_map/ppermute | solution.py:22
  56.8 1.9 collective-permute-start
  57.8 27.0 %copy-start.6 = (bf16[1,4,4,32,128]{4,3,2,1,0:T(8,128)(2,1)S(1)}, bf16[1,4,4,32,128]{4,3,2,1,0:T(8,128)(2,1)}, u32[]{:S(2)}) copy-start(bf16[1,4,4,32,128]{4,3,2,1,0:T(8,128)(2,1)} %get-tuple-element.86) | copy-start | bytes 393220
  57.8 35.8 %copy-start.5 = (bf16[1,4,4,32,128]{4,3,2,1,0:T(8,128)(2,1)S(1)}, bf16[1,4,4,32,128]{4,3,2,1,0:T(8,128)(2,1)}, u32[]{:S(2)}) copy-start(bf16[1,4,4,32,128]{4,3,2,1,0:T(8,128)(2,1)} %get-tuple-element.85) | copy-start | bytes 393220
  57.8 40.0 %copy-start.4 = (bf16[1,4,4,32,128]{4,3,2,1,0:T(8,128)(2,1)S(1)}, bf16[1,4,4,32,128]{4,3,2,1,0:T(8,128)(2,1)}, u32[]{:S(2)}) copy-start(bf16[1,4,4,32,128]{4,3,2,1,0:T(8,128)(2,1)} %get-tuple-element.84) | copy-start | bytes 393220
  58.6 9.9 %collective-permute-start.2 = (bf16[1,4,4,32,128]{4,3,2,1,0:T(8,128)(2,1)}, bf16[1,4,4,32,128]{4,3,2,1,0:T(8,128)(2,1)S(1)}, u32[]{:S(2)}, u32[]{:S(2)}) collective-permute-start(bf16[1,4,4,32,128]{4,3,2,1,0:T(8,128)(2,1)} %get-tuple-element.93), channel_id=1, source_target_pairs={{0,6},{2,4},{4,2},{6,0},{8,14},{10,12},{12,10},{14,8},{16,22},{18,... | collective-permute-start | bytes 393224 | tf_op jit(solution)/shard_map/ppermute | solution.py:22
  61.9 8.7 %collective-permute-start.3 = (bf16[1,4,4,32,128]{4,3,2,1,0:T(8,128)(2,1)}, bf16[1,4,4,32,128]{4,3,2,1,0:T(8,128)(2,1)S(1)}, u32[]{:S(2)}, u32[]{:S(2)}) collective-permute-start(bf16[1,4,4,32,128]{4,3,2,1,0:T(8,128)(2,1)} %get-tuple-element.92), channel_id=1, source_target_pairs={{0,8},{2,10},{4,12},{6,14},{8,0},{10,2},{12,4},{14,6},{16,24},{18,... | collective-permute-start | bytes 393224 | tf_op jit(solution)/shard_map/ppermute | solution.py:22
  68.5 6.0 %collective-permute-start.4 = (bf16[1,4,4,32,128]{4,3,2,1,0:T(8,128)(2,1)}, bf16[1,4,4,32,128]{4,3,2,1,0:T(8,128)(2,1)S(1)}, u32[]{:S(2)}, u32[]{:S(2)}) collective-permute-start(bf16[1,4,4,32,128]{4,3,2,1,0:T(8,128)(2,1)} %get-tuple-element.91), channel_id=1, source_target_pairs={{0,10},{2,8},{4,14},{6,12},{8,2},{10,0},{12,6},{14,4},{16,26},{18,... | collective-permute-start | bytes 393224 | tf_op jit(solution)/shard_map/ppermute | solution.py:22
  70.6 8.1 %collective-permute-start.5 = (bf16[1,4,4,32,128]{4,3,2,1,0:T(8,128)(2,1)}, bf16[1,4,4,32,128]{4,3,2,1,0:T(8,128)(2,1)S(1)}, u32[]{:S(2)}, u32[]{:S(2)}) collective-permute-start(bf16[1,4,4,32,128]{4,3,2,1,0:T(8,128)(2,1)} %get-tuple-element.90), channel_id=1, source_target_pairs={{0,12},{2,14},{4,8},{6,10},{8,4},{10,6},{12,0},{14,2},{16,28},{18,... | collective-permute-start | bytes 393224 | tf_op jit(solution)/shard_map/ppermute | solution.py:22
  74.5 7.2 %collective-permute-start.6 = (bf16[1,4,4,32,128]{4,3,2,1,0:T(8,128)(2,1)}, bf16[1,4,4,32,128]{4,3,2,1,0:T(8,128)(2,1)S(1)}, u32[]{:S(2)}, u32[]{:S(2)}) collective-permute-start(bf16[1,4,4,32,128]{4,3,2,1,0:T(8,128)(2,1)} %get-tuple-element.89), channel_id=1, source_target_pairs={{0,14},{2,12},{4,10},{6,8},{8,6},{10,4},{12,2},{14,0},{16,30},{18,... | collective-permute-start | bytes 393224 | tf_op jit(solution)/shard_map/ppermute | solution.py:22
  78.7 6.1 %collective-permute-start.7 = (bf16[1,4,4,32,128]{4,3,2,1,0:T(8,128)(2,1)}, bf16[1,4,4,32,128]{4,3,2,1,0:T(8,128)(2,1)S(1)}, u32[]{:S(2)}, u32[]{:S(2)}) collective-permute-start(bf16[1,4,4,32,128]{4,3,2,1,0:T(8,128)(2,1)} %get-tuple-element.88), channel_id=1, source_target_pairs={{0,16},{2,18},{4,20},{6,22},{8,24},{10,26},{12,28},{14,30},{16,0},... | collective-permute-start | bytes 393224 | tf_op jit(solution)/shard_map/ppermute | solution.py:22
  81.7 12.0 %collective-permute-start.8 = (bf16[1,4,4,32,128]{4,3,2,1,0:T(8,128)(2,1)}, bf16[1,4,4,32,128]{4,3,2,1,0:T(8,128)(2,1)S(1)}, u32[]{:S(2)}, u32[]{:S(2)}) collective-permute-start(bf16[1,4,4,32,128]{4,3,2,1,0:T(8,128)(2,1)} %get-tuple-element.87), channel_id=1, source_target_pairs={{0,18},{2,16},{4,22},{6,20},{8,26},{10,24},{12,30},{14,28},{16,2},... | collective-permute-start | bytes 393224 | tf_op jit(solution)/shard_map/ppermute | solution.py:22
  84.8 13.1 %collective-permute-start.9 = (bf16[1,4,4,32,128]{4,3,2,1,0:T(8,128)(2,1)S(1)}, bf16[1,4,4,32,128]{4,3,2,1,0:T(8,128)(2,1)S(1)}, u32[]{:S(2)}, u32[]{:S(2)}) collective-permute-start(bf16[1,4,4,32,128]{4,3,2,1,0:T(8,128)(2,1)S(1)} %copy-done.6), channel_id=1, source_target_pairs={{0,20},{2,22},{4,16},{6,18},{8,28},{10,30},{12,24},{14,26},{16,4},... | collective-permute-start | bytes 393224 | tf_op jit(solution)/shard_map/ppermute | solution.py:22
  93.6 31.3 %copy-start.8 = (pred[4,8]{1,0:T(4,128)(4,1)S(1)}, pred[4,8]{1,0:T(4,128)(4,1)}, u32[]{:S(2)}) copy-start(pred[4,8]{1,0:T(4,128)(4,1)} %broadcast_in_dim.201) | copy-start | bytes 100
  93.6 8.5 %collective-permute-start.10 = (bf16[1,4,4,32,128]{4,3,2,1,0:T(8,128)(2,1)S(1)}, bf16[1,4,4,32,128]{4,3,2,1,0:T(8,128)(2,1)S(1)}, u32[]{:S(2)}, u32[]{:S(2)}) collective-permute-start(bf16[1,4,4,32,128]{4,3,2,1,0:T(8,128)(2,1)S(1)} %copy-done.5), channel_id=1, source_target_pairs={{0,22},{2,20},{4,18},{6,16},{8,30},{10,28},{12,26},{14,24},{16,6},... | collective-permute-start | bytes 393224 | tf_op jit(solution)/shard_map/ppermute | solution.py:22
  97.8 10.1 %collective-permute-start.11 = (bf16[1,4,4,32,128]{4,3,2,1,0:T(8,128)(2,1)S(1)}, bf16[1,4,4,32,128]{4,3,2,1,0:T(8,128)(2,1)S(1)}, u32[]{:S(2)}, u32[]{:S(2)}) collective-permute-start(bf16[1,4,4,32,128]{4,3,2,1,0:T(8,128)(2,1)S(1)} %copy-done.4), channel_id=1, source_target_pairs={{0,24},{2,26},{4,28},{6,30},{8,16},{10,18},{12,20},{14,22},{16,8},... | collective-permute-start | bytes 393224 | tf_op jit(solution)/shard_map/ppermute | solution.py:22
  113.2 23.7 %copy-start.3 = (f32[4,8,4,128]{3,2,1,0:T(4,128)S(1)}, f32[4,8,4,128]{3,2,1,0:T(4,128)}, u32[]{:S(2)}) copy-start(f32[4,8,4,128]{3,2,1,0:T(4,128)} %custom-call.22) | copy-start | bytes 196612
  116.5 13.6 %all-to-all-start.2 = ((f32[16,4,4,128]{3,2,1,0:T(4,128)}), f32[16,4,4,128]{3,2,1,0:T(4,128)S(1)}, u32[]{:S(2)}, u32[]{:S(2)}) async-start(f32[16,4,4,128]{3,2,1,0:T(4,128)} %bitcast.24), calls=%async_computation.2 | async-start | bytes 262144 | tf_op jit(solution)/shard_map/all_to_all | solution.py:114
  130.1 27.9 %all-to-all-start = ((f32[16,1,4]{2,1,0:T(1,128)}), f32[16,1,4]{2,1,0:T(1,128)S(1)}, u32[]{:S(2)}, u32[]{:S(2)}) async-start(f32[16,1,4]{2,1,0:T(1,128)} %copy.61), calls=%async_computation | async-start | bytes 16384 | tf_op jit(solution)/shard_map/all_to_all | solution.py:160
  137.0 20.2 %copy-start.9 = (pred[64]{0:T(512)(128)(4,1)S(1)}, pred[64]{0:T(512)(128)(4,1)}, u32[]{:S(2)}) copy-start(pred[64]{0:T(512)(128)(4,1)} %compare_and_fusion) | copy-start | bytes 196
  158.1 11.2 %all-to-all-start.5 = ((f32[16,4,4,128]{3,2,1,0:T(4,128)}), f32[16,4,4,128]{3,2,1,0:T(4,128)S(1)}, u32[]{:S(2)}, u32[]{:S(2)}) async-start(f32[16,4,4,128]{3,2,1,0:T(4,128)} %bitcast.40), calls=%async_computation.5 | async-start | bytes 262144 | tf_op jit(solution)/shard_map/all_to_all | solution.py:158
  169.3 11.4 %all-to-all-start.7 = ((f32[16,4,4,128]{3,2,1,0:T(4,128)}), f32[16,4,4,128]{3,2,1,0:T(4,128)S(1)}, u32[]{:S(2)}, u32[]{:S(2)}) async-start(f32[16,4,4,128]{3,2,1,0:T(4,128)} %bitcast.46), calls=%async_computation.7 | async-start | bytes 262144 | tf_op jit(solution)/shard_map/all_to_all | solution.py:159
  180.7 99.6 %all-to-all-start.6 = ((f32[16,4,4,32,128]{4,3,2,1,0:T(8,128)}), f32[16,4,4,32,128]{4,3,2,1,0:T(8,128)}, u32[]{:S(2)}, u32[]{:S(2)}) async-start(f32[16,4,4,32,128]{4,3,2,1,0:T(8,128)} %select_select_fusion), calls=%async_computation.6 | async-start | bytes 8388608 | tf_op jit(solution)/shard_map/all_to_all | solution.py:157
  294.2 1.0 copy-start.2
  294.2 1.0 copy-start.7
Sparse Core Ops, SparseCore 0:
  8.9 22.2 all-gather.1
